TPU v7x, 32 devices: a whole 2x2x4 slice. The times are simulated.
32 devices in a mesh: dp: 4 (over y, core), vocab: 8 (over z, x).
Axes of the slice: x: 2, y: 2, z: 4, core: 2. Of those that a mesh axis runs over, the one named last changes fastest.
Arguments:
- hidden: bfloat16 [768, 8192], P('dp', 'vocab'), may hold values from -100 to 100
- proj: bfloat16 [8192, 65536], P(None, ('dp', 'vocab')), may hold values from -3 to 3
- target_ids: int32 [768], replicated, may hold values from 0 to 65535
- seq_len: int32 [16], replicated, may hold values from 1 to 189, as said below
- seq_way: int32 [16], replicated, may hold values from 0 to 3
Outputs:
- token_logprob: float32 [768], P('dp')
- token_entropy: float32 [768], P('dp')
- seq_logprob: float32 [16], replicated
Inputs may be any that keep to these rules, and one draw needn't show every extreme that they name: `seq_len`: each data way is given exactly 4 sequences, which fill its first slots one after another in increasing sequence number; the lengths on one way add up to at most 192, to exactly 192 on some way, and over all ways to exactly 372. Some sequence has exactly 189 tokens.
All inputs are finite; a program needn't handle non-finite values.
Results may differ from a plain program's by a relative error of at most 0.0003.
Values may be sent and summed in bfloat16 or wider, within the bound.
No kernel may reach another device: no remote copies, remote signals or barrier semaphores. Data moves between devices by JAX's collectives and lax.ppermute only.
A program may use at most 128 MiB of HBM per device.

v0:
```python
import jax
import jax.numpy as jnp
from jax import lax
from jax.sharding import PartitionSpec as P


def membership(seq_len, seq_way, slots, ways):
    count = seq_len.shape[0]
    order = jnp.arange(count, dtype=jnp.int32)
    earlier = (seq_way[:, None] == seq_way[None, :]) & (order[:, None] < order[None, :])
    start = jnp.sum(jnp.where(earlier, seq_len[:, None], 0), axis=0)
    row = jnp.arange(slots * ways, dtype=jnp.int32)
    owner = row // slots
    within = row % slots
    return (
        (seq_way[None, :] == owner[:, None])
        & (within[:, None] >= start[None, :])
        & (within[:, None] < (start + seq_len)[None, :])
    )


def target_logit(logits, first_col, targets):
    columns = first_col + jnp.arange(logits.shape[1], dtype=jnp.int32)
    return jnp.sum(jnp.where(targets[:, None] == columns[None, :], logits, 0.0), axis=1)


def per_device(hidden, proj, target_ids, seq_len, seq_way):
    ways = lax.axis_size("dp")
    slots = hidden.shape[0]
    width = proj.shape[1]
    first_col = (lax.axis_index("dp") * lax.axis_size("vocab") + lax.axis_index("vocab")) * width
    member = membership(seq_len, seq_way, slots, ways)
    valid = jnp.any(member, axis=1)
    kept = slots + (ways - 1) * (5 * slots // 16)
    source = jnp.nonzero(valid, size=kept)[0].astype(jnp.int32)
    slot_rows = lax.all_gather(hidden, "dp", axis=0, tiled=True)
    slot_rows = jnp.take(slot_rows, source, axis=0)
    empty = jnp.zeros((slot_rows.shape[0], width), jnp.float32)
    piece = lax.all_gather(slot_rows, "vocab", axis=1, tiled=True)
    weights_part = lax.slice_in_dim(proj, 0, piece.shape[1], axis=0)
    logits = empty + jnp.dot(piece, weights_part, preferred_element_type=jnp.float32)
    targets = jnp.take(target_ids, source)
    top = lax.pmax(jnp.max(logits, axis=1), ("dp", "vocab"))
    shifted = logits - top[:, None]
    weight = jnp.exp(shifted)
    partial_total = jnp.sum(weight, axis=1)
    partial_moment = jnp.sum(weight * shifted, axis=1)
    partial_pick = target_logit(logits, first_col, targets)
    total, moment, picked = lax.psum((partial_total, partial_moment, partial_pick), ("dp", "vocab"))
    log_total = jnp.log(total)
    logprob = picked - top - log_total
    entropy = log_total - moment / total
    position = jnp.clip(jnp.cumsum(valid.astype(jnp.int32)) - 1, 0, kept - 1)
    logprob = jnp.take(logprob, position)
    entropy = jnp.take(entropy, position)
    logprob = jnp.where(valid, logprob, 0.0)
    entropy = jnp.where(valid, entropy, 0.0)
    seq_logprob = jnp.dot(member.astype(jnp.float32).T, logprob, precision=lax.Precision.HIGHEST)
    mine = lax.axis_index("dp") * slots
    return (
        lax.dynamic_slice_in_dim(logprob, mine, slots),
        lax.dynamic_slice_in_dim(entropy, mine, slots),
        seq_logprob,
    )


def solution(mesh):
    placed = (P("dp", "vocab"), P(None, ("dp", "vocab")), P(), P(), P())
    return jax.shard_map(
        per_device, mesh=mesh, in_specs=placed, out_specs=(P("dp"), P("dp"), P()), check_vma=False
    )
```

profile of v0, /device:TPU:0, one launch (start us, length us, event | category | flops | bytes accessed | tf_op | source)
XLA Modules:
  0.0 252.8 jit_solution(5199935121972603821)
XLA Ops:
  7.2 0.0 copy-start
  7.2 0.0 all-gather.3.cloned.1.call-start
  7.2 0.7 all-gather.3.cloned.1.call-update
  7.9 0.0 all-gather.5.cloned.1.call-start
  8.0 0.8 select_reduce_fusion.1
  8.8 0.7 add.90
  9.4 0.8 and_reduce_fusion
  10.2 0.3 reduce-window.16
  10.5 0.1 slice.15
  10.6 0.1 slice_reduce_fusion
  10.7 0.1 add_bitcast_fusion
  10.8 5.8 %scatter_custom_fusion = s32[372]{0:T(512)S(1)} fusion(s32[768]{0:T(1024)S(1)} %fusion.17, s32[768]{0:T(1024)S(1)} %ne.69, s32[]{:T(128)} %constant.99.clone.1), kind=kCustom, calls=%fused_computation.60 | custom fusion | flops 768 | bytes 1492 | tf_op jit(solution)/shard_map/scatter-add | solution.py:35
  16.7 0.3 reduce-window.24
  17.0 0.1 slice.17
  17.1 0.6 convert_reduce_fusion
  17.7 0.1 slice_reduce_fusion.1
  17.9 0.1 add_bitcast_fusion.1
  17.9 0.7 compare_select_fusion.2
  18.6 0.0 copy-done
  18.6 1.9 gather_fusion
  20.5 0.7 broadcast_select_fusion.1
  21.2 10.8 %all-gather.3.cloned.1.call-done = bf16[768,1024]{1,0:T(8,128)(2,1)} async-done(((bf16[192,1024]{1,0:T(8,128)(2,1)}), bf16[768,1024]{1,0:T(8,128)(2,1)}) %all-gather.3.cloned.1.call-update) | async-done | bytes 1572880 | tf_op jit(solution)/shard_map/all_gather | solution.py:36
  32.0 4.4 %gather_fusion.1 = bf16[372,1024]{1,0:T(8,128)(2,1)S(1)} fusion(bf16[768,1024]{1,0:T(8,128)(2,1)} %all-gather.3.cloned.1.call-done, s32[1024]{0:T(1024)S(1)} %pad_clamp_fusion.1), kind=kCustom, calls=%fused_computation.3 | custom fusion | bytes 1525200 | tf_op jit(solution)/shard_map/jit(_take)/gather | solution.py:37
  36.4 1.0 broadcast_select_fusion
  37.4 0.0 all-gather.5.cloned.1.call-update
  37.5 0.1 compare_select_fusion.1
  37.6 97.1 %all-gather.5.cloned.1.call-done = bf16[372,8192]{1,0:T(8,128)(2,1)} async-done(((bf16[372,1024]{1,0:T(8,128)(2,1)}), bf16[372,8192]{1,0:T(8,128)(2,1)}) %all-gather.5.cloned.1.call-update) | async-done | bytes 6094864 | tf_op jit(solution)/shard_map/all_gather | solution.py:39
  134.7 18.9 %fusion.21 = (f32[372]{0:T(512)S(1)}, f32[372,2048]{1,0:T(8,128)S(1)}) fusion(bf16[372,8192]{1,0:T(8,128)(2,1)} %all-gather.5.cloned.1.call-done, bf16[8192,2048]{1,0:T(8,128)(2,1)} %param.8), kind=kOutput, calls=%fused_computation.62 | convolution fusion | flops 12483010560 | bytes 42698192 | tf_op jit(solution)/shard_map/dot_general | solution.py:41
  153.6 38.4 %pmax.7 = f32[372]{0:T(512)S(1)} all-reduce(f32[372]{0:T(512)S(1)} %get-tuple-element.16), channel_id=1, replica_groups=mesh['dp'=4,'vocab'=8] {'dp','vocab'}, use_global_device_ids=true, to_apply=%region_11.12 | all-reduce | flops 372 | bytes 2976 | tf_op jit(solution)/shard_map/pmax | solution.py:43
  192.0 1.1 fusion
  193.1 40.8 %all-reduce.1 = (f32[372]{0:T(512)S(1)}, f32[372]{0:T(512)S(1)}, f32[372]{0:T(512)S(1)}) all-reduce(f32[372]{0:T(512)S(1)} %get-tuple-element.6, f32[372]{0:T(512)S(1)} %get-tuple-element.5, f32[372]{0:T(512)S(1)} %get-tuple-element.4), channel_id=1, replica_groups=mesh['dp'=4,'vocab'=8] {'dp','vocab'}, use_global_device_ids=true, to_apply=%region_9.10 | all-reduce | flops 1116 | bytes 8928 | tf_op jit(solution)/shard_map/psum | solution.py:49
  233.9 5.0 %gather_fusion.2 = f32[768]{0:T(1024)S(1)} fusion(f32[372]{0:T(512)S(1)} %get-tuple-element.14, s32[1024]{0:T(1024)S(1)} %pad_clamp_fusion), kind=kCustom, calls=%fused_computation.clone | custom fusion | bytes 9216 | tf_op jit(solution)/shard_map/jit(_take)/gather | solution.py:54
  238.9 0.0 copy-start.1
  238.9 5.0 %gather_fusion.3 = f32[768]{0:T(1024)S(1)} fusion(f32[372]{0:T(512)S(1)} %get-tuple-element.15, s32[1024]{0:T(1024)S(1)} %pad_clamp_fusion), kind=kCustom, calls=%fused_computation.1.clone | custom fusion | bytes 9216 | tf_op jit(solution)/shard_map/jit(_take)/gather | solution.py:55
  244.0 0.0 copy-done.1
  244.0 0.7 convolution_bitcast_fusion
  244.7 0.6 dynamic_slice.6
  245.4 0.6 dynamic_slice.7
  (14 shorter events, 0.1 us)
Async XLA Ops:
  7.2 11.5 %copy-start = (s32[768]{0:T(1024)S(1)}, s32[768]{0:T(1024)}, u32[]{:S(2)}) copy-start(s32[768]{0:T(1024)} %param.9) | copy-start | bytes 9220
  7.2 24.8 %all-gather.3.cloned.1.call-start = ((), (), s32[]{:S(2)}) async-start(), calls=%async_computation | async-start | bytes 1966080 | tf_op jit(solution)/shard_map/all_gather | solution.py:36
  7.9 126.8 %all-gather.5.cloned.1.call-start = ((), (), s32[]{:S(2)}) async-start(), calls=%async_computation.1 | async-start | bytes 6930432 | tf_op jit(solution)/shard_map/all_gather | solution.py:39
  238.9 5.1 %copy-start.1 = (s32[16]{0:T(128)S(1)}, s32[16]{0:T(128)}, u32[]{:S(2)}) copy-start(s32[16]{0:T(128)} %param.11) | copy-start | bytes 196
Sparse Core Ops, SparseCore 0:
  9.5 22.3 all-gather.2
  37.6 97.0 all-gather.4
where the time goes:
time: 253 us
  waiting for transfers between devices  109 us (43%)
  blocking collectives  79.2 us (31%)
  matrix products  19.6 us (8%)
  local copies, waits for them, and re-layouts  18 us (7%)
  between operations  14.2 us (6%)
  other arithmetic  13.1 us (5%)
    all_gather x1, waiting for transfers between devices, per_device(): piece = lax.all_gather(slot_rows, 'vocab', axis=1, tiled=True)  97.1 us
    psum x1, blocking collectives, per_device(): lax.psum((partial_total, partial_moment, partial_pick), ('dp', 'vocab'))  40.8 us
    pmax x1, blocking collectives, per_device(): top = lax.pmax(jnp.max(logits, axis=1), ('dp', 'vocab'))  38.4 us
    dot_general x1, matrix products, per_device(): jnp.dot(piece, weights_part, preferred_element_type=jnp.float32)  18.9 us
    all_gather x1, waiting for transfers between devices, per_device(): slot_rows = lax.all_gather(hidden, 'dp', axis=0, tiled=True)  10.8 us
    scatter-add x1, other arithmetic, per_device(): source = jnp.nonzero(valid, size=kept)[0].astype(jnp.int32)  5.85 us
  transfers between devices with their start and end apart: 2, of which 2 were waited for; matrix products, arithmetic and copies ran while one was open for 5% of the time, Pallas kernels for 0%

commit v1 on v0

--- a/solution.py
+++ b/solution.py
@@ -2,6 +2,12 @@
 import jax.numpy as jnp
 from jax import lax
 from jax.sharding import PartitionSpec as P
+
+
+def direct_view(v0):
+    for rr in ("vocab", "dp"):
+        v0 = lax.psum(v0, rr)
+    return v0
 
 
 def membership(seq_len, seq_way, slots, ways):
@@ -46,7 +52,7 @@
     partial_total = jnp.sum(weight, axis=1)
     partial_moment = jnp.sum(weight * shifted, axis=1)
     partial_pick = target_logit(logits, first_col, targets)
-    total, moment, picked = lax.psum((partial_total, partial_moment, partial_pick), ("dp", "vocab"))
+    total, moment, picked = direct_view((partial_total, partial_moment, partial_pick))
     log_total = jnp.log(total)
     logprob = picked - top - log_total
     entropy = log_total - moment / total

time: 253 us -> 240 us (0.949)
  blocking collectives: 79.2 us -> 65.5 us
    psum x1 -> x2, blocking collectives: 40.8 us -> 27.1 us  [direct_view(): v0 = lax.psum(v0, rr)]
  transfers between devices with their start and end apart: 2 -> 2, of which waited for: 2 -> 2; matrix products, arithmetic and copies ran while one was open for 5% -> 6% of each run, Pallas kernels for 0% -> 0%
where the time goes in v1:
time: 240 us; the launch traced here: 239 us
  waiting for transfers between devices  109 us (45%)
  blocking collectives  65.5 us (27%)
  matrix products  19.6 us (8%)
  local copies, waits for them, and re-layouts  18 us (8%)
  between operations  14.2 us (6%)
  other arithmetic  13.1 us (5%)
    all_gather x1, waiting for transfers between devices, per_device(): piece = lax.all_gather(slot_rows, 'vocab', axis=1, tiled=True)  97.1 us
    pmax x1, blocking collectives, per_device(): top = lax.pmax(jnp.max(logits, axis=1), ('dp', 'vocab'))  38.4 us
    psum x2, blocking collectives, direct_view(): v0 = lax.psum(v0, rr)  27.1 us
    dot_general x1, matrix products, per_device(): jnp.dot(piece, weights_part, preferred_element_type=jnp.float32)  18.9 us
    all_gather x1, waiting for transfers between devices, per_device(): slot_rows = lax.all_gather(hidden, 'dp', axis=0, tiled=True)  10.8 us
    scatter-add x1, other arithmetic, per_device(): source = jnp.nonzero(valid, size=kept)[0].astype(jnp.int32)  5.85 us
    gather x1, local copies, waits for them, and re-layouts, per_device(): entropy = jnp.take(entropy, position)  5.01 us
    gather x1, local copies, waits for them, and re-layouts, per_device(): logprob = jnp.take(logprob, position)  5.01 us
  transfers between devices with their start and end apart: 2, of which 2 were waited for; matrix products, arithmetic and copies ran while one was open for 6% of the time, Pallas kernels for 0%

profile of v1, /device:TPU:0, one launch (start us, length us, event | category | flops | bytes accessed | tf_op | source)
XLA Modules:
  0.0 239.1 jit_solution(5951062352761225107)
XLA Ops:
  7.2 0.0 copy-start
  7.2 0.0 all-gather.3.cloned.1.call-start
  7.2 0.7 all-gather.3.cloned.1.call-update
  7.9 0.0 all-gather.5.cloned.1.call-start
  8.0 0.8 select_reduce_fusion.1
  8.8 0.7 add.96
  9.4 0.8 and_reduce_fusion
  10.2 0.3 reduce-window.16
  10.5 0.1 slice.15
  10.6 0.1 slice_reduce_fusion
  10.7 0.1 add_bitcast_fusion
  10.8 5.8 %scatter_custom_fusion = s32[372]{0:T(512)S(1)} fusion(s32[768]{0:T(1024)S(1)} %fusion.17, s32[768]{0:T(1024)S(1)} %ne.69, s32[]{:T(128)} %constant.99.clone.1), kind=kCustom, calls=%fused_computation.60 | custom fusion | flops 768 | bytes 1492 | tf_op jit(solution)/shard_map/scatter-add | solution.py:41
  16.7 0.3 reduce-window.24
  17.0 0.1 slice.17
  17.1 0.6 convert_reduce_fusion
  17.7 0.1 slice_reduce_fusion.1
  17.9 0.1 add_bitcast_fusion.1
  17.9 0.7 compare_select_fusion.2
  18.6 0.0 copy-done
  18.6 1.9 gather_fusion
  20.5 0.7 broadcast_select_fusion.1
  21.2 10.8 %all-gather.3.cloned.1.call-done = bf16[768,1024]{1,0:T(8,128)(2,1)} async-done(((bf16[192,1024]{1,0:T(8,128)(2,1)}), bf16[768,1024]{1,0:T(8,128)(2,1)}) %all-gather.3.cloned.1.call-update) | async-done | bytes 1572880 | tf_op jit(solution)/shard_map/all_gather | solution.py:42
  32.0 4.4 %gather_fusion.1 = bf16[372,1024]{1,0:T(8,128)(2,1)S(1)} fusion(bf16[768,1024]{1,0:T(8,128)(2,1)} %all-gather.3.cloned.1.call-done, s32[1024]{0:T(1024)S(1)} %pad_clamp_fusion.1), kind=kCustom, calls=%fused_computation.3 | custom fusion | bytes 1525200 | tf_op jit(solution)/shard_map/jit(_take)/gather | solution.py:43
  36.4 1.0 broadcast_select_fusion
  37.4 0.0 all-gather.5.cloned.1.call-update
  37.5 0.1 compare_select_fusion.1
  37.6 97.1 %all-gather.5.cloned.1.call-done = bf16[372,8192]{1,0:T(8,128)(2,1)} async-done(((bf16[372,1024]{1,0:T(8,128)(2,1)}), bf16[372,8192]{1,0:T(8,128)(2,1)}) %all-gather.5.cloned.1.call-update) | async-done | bytes 6094864 | tf_op jit(solution)/shard_map/all_gather | solution.py:45
  134.7 18.9 %fusion.21 = (f32[372]{0:T(512)S(1)}, f32[372,2048]{1,0:T(8,128)S(1)}) fusion(bf16[372,8192]{1,0:T(8,128)(2,1)} %all-gather.5.cloned.1.call-done, bf16[8192,2048]{1,0:T(8,128)(2,1)} %param.8), kind=kOutput, calls=%fused_computation.62 | convolution fusion | flops 12483010560 | bytes 42698192 | tf_op jit(solution)/shard_map/dot_general | solution.py:47
  153.6 38.4 %pmax.7 = f32[372]{0:T(512)S(1)} all-reduce(f32[372]{0:T(512)S(1)} %get-tuple-element.19), channel_id=1, replica_groups=mesh['dp'=4,'vocab'=8] {'dp','vocab'}, use_global_device_ids=true, to_apply=%region_12.13 | all-reduce | flops 372 | bytes 2976 | tf_op jit(solution)/shard_map/pmax | solution.py:49
  192.0 1.1 fusion
  193.1 21.3 %all-reduce.1 = (f32[372]{0:T(512)S(1)}, f32[372]{0:T(512)S(1)}, f32[372]{0:T(512)S(1)}) all-reduce(f32[372]{0:T(512)S(1)} %get-tuple-element.6, f32[372]{0:T(512)S(1)} %get-tuple-element.5, f32[372]{0:T(512)S(1)} %get-tuple-element.4), channel_id=1, replica_groups=mesh['dp'=4,'vocab'=8] {'vocab'}, use_global_device_ids=true, to_apply=%region_9.10 | all-reduce | flops 1116 | bytes 8928 | tf_op jit(solution)/shard_map/psum | solution.py:9
  214.4 5.7 %all-reduce.2 = (f32[372]{0:T(512)S(1)}, f32[372]{0:T(512)S(1)}, f32[372]{0:T(512)S(1)}) all-reduce(f32[372]{0:T(512)S(1)} %get-tuple-element.7, f32[372]{0:T(512)S(1)} %get-tuple-element.8, f32[372]{0:T(512)S(1)} %get-tuple-element.9), channel_id=1, replica_groups=mesh['dp'=4,'vocab'=8] {'dp'}, use_global_device_ids=true, to_apply=%region_10.11 | all-reduce | flops 1116 | bytes 8928 | tf_op jit(solution)/shard_map/psum | solution.py:9
  220.2 5.0 %gather_fusion.2 = f32[768]{0:T(1024)S(1)} fusion(f32[372]{0:T(512)S(1)} %get-tuple-element.17, s32[1024]{0:T(1024)S(1)} %pad_clamp_fusion), kind=kCustom, calls=%fused_computation.clone | custom fusion | bytes 9216 | tf_op jit(solution)/shard_map/jit(_take)/gather | solution.py:60
  225.2 0.0 copy-start.1
  225.2 5.0 %gather_fusion.3 = f32[768]{0:T(1024)S(1)} fusion(f32[372]{0:T(512)S(1)} %get-tuple-element.18, s32[1024]{0:T(1024)S(1)} %pad_clamp_fusion), kind=kCustom, calls=%fused_computation.1.clone | custom fusion | bytes 9216 | tf_op jit(solution)/shard_map/jit(_take)/gather | solution.py:61
  230.3 0.0 copy-done.1
  230.3 0.7 convolution_bitcast_fusion
  231.0 0.6 dynamic_slice.6
  231.7 0.6 dynamic_slice.7
  (14 shorter events, 0.1 us)
Async XLA Ops:
  7.2 11.5 %copy-start = (s32[768]{0:T(1024)S(1)}, s32[768]{0:T(1024)}, u32[]{:S(2)}) copy-start(s32[768]{0:T(1024)} %param.9) | copy-start | bytes 9220
  7.2 24.8 %all-gather.3.cloned.1.call-start = ((), (), s32[]{:S(2)}) async-start(), calls=%async_computation | async-start | bytes 1966080 | tf_op jit(solution)/shard_map/all_gather | solution.py:42
  7.9 126.8 %all-gather.5.cloned.1.call-start = ((), (), s32[]{:S(2)}) async-start(), calls=%async_computation.1 | async-start | bytes 6930432 | tf_op jit(solution)/shard_map/all_gather | solution.py:45
  225.2 5.1 %copy-start.1 = (s32[16]{0:T(128)S(1)}, s32[16]{0:T(128)}, u32[]{:S(2)}) copy-start(s32[16]{0:T(128)} %param.11) | copy-start | bytes 196
Sparse Core Ops, SparseCore 0:
  9.5 22.3 all-gather.2
  37.6 97.0 all-gather.4
